TPU v7x, 512 devices: a 8x2x16 block of a 8x16x16 slice. The times are simulated.
512 devices in a mesh: parts: 2 (over y), blk: 16 (over z), sub: 8 (over x), rep: 2 (over core).
Axes of the slice: x: 8, y: 2, z: 16, core: 2. Of those that a mesh axis runs over, the one named last changes fastest.
The devices are a block of a 8x16x16 slice.
Arguments:
- queries: bfloat16 [2048, 32, 128], P(('parts', 'blk', 'sub', 'rep')), parts along dimension 0, may hold values from -1.5 to 1.5
- passages: bfloat16 [2048, 128, 128], P(('parts', 'blk')), parts along dimension 0, may hold values from -1.5 to 1.5
- lengths: int32 [2048], P(('parts', 'blk')), parts along dimension 0, may hold values from 8 to 128
- slot_of: int32 [2048], P('parts'), parts along dimension 0, may hold values from 0 to 1023, each once
- candidates: int32 [2048, 256], P(('parts', 'blk', 'sub', 'rep')), parts along dimension 0, may hold values from 0 to 1023
Outputs:
- score: float32 [2048, 256], P(('parts', 'blk', 'sub', 'rep')), parts along dimension 0
- top: float32 [2048, 10], P(('parts', 'blk', 'sub', 'rep')), parts along dimension 0
There are 2 independent parts, one for each index of `parts`. A program takes and returns all parts, laid end to end along the dimension named above; each array names one. Nothing has to cross between parts.
Inputs may be any that keep to these rules, and one draw needn't show every extreme that they name: `slot_of`: a permutation; storage row r lies on the blk index r // 64. `candidates`: passage ids, repeats allowed. `lengths`: the live slots of a row are its first ones.
All inputs are finite; a program needn't handle non-finite values.
Results may differ from a plain program's by a relative error of at most 0.0003.
Values may be sent and summed in bfloat16 or wider, within the bound.
A program may use at most 64 MiB of HBM per device.

v0:
```python
import jax
import jax.numpy as jnp
from jax import lax
from jax.sharding import PartitionSpec as P

TOPN = 10


def score_table(rows_q, passages, lengths):
    queries_here = rows_q.shape[0]
    tokens = rows_q.shape[1]
    width = rows_q.shape[2]
    count = passages.shape[0]
    span = passages.shape[1]
    group = 4
    flat = rows_q.reshape(queries_here * tokens, width)
    blocks = passages.reshape(count // group, group * span, width)
    spans = lengths.reshape(count // group, group)

    def one_block(pair):
        piece, live_count = pair
        similar = lax.dot_general(
            flat, piece, (((1,), (1,)), ((), ())), preferred_element_type=jnp.float32
        )
        similar = similar.reshape(queries_here * tokens, group, span)
        live = lax.broadcasted_iota(jnp.int32, (group, span), 1) < live_count[:, None]
        best = jnp.max(jnp.where(live[None], similar, -1e30), axis=2)
        return jnp.sum(best.reshape(queries_here, tokens, group), axis=1) / tokens

    table = lax.map(one_block, (blocks, spans))
    return jnp.transpose(table, (1, 0, 2)).reshape(queries_here, count)


def shards(queries, passages, lengths, slot_of, candidates):
    table = score_table(lax.all_gather(queries, "blk", axis=0, tiled=True), passages, lengths)
    whole = lax.all_to_all(table, "blk", split_axis=0, concat_axis=1, tiled=True)
    score = jnp.take_along_axis(whole, jnp.take(slot_of, candidates, axis=0), axis=1)
    top = lax.top_k(score, TOPN)[0]
    return (score, top)


def solution(mesh):
    return jax.shard_map(
        shards,
        mesh=mesh,
        in_specs=(
            P(("parts", "blk", "sub", "rep"), None, None),
            P(("parts", "blk"), None, None),
            P(("parts", "blk")),
            P("parts"),
            P(("parts", "blk", "sub", "rep"), None),
        ),
        out_specs=(
            P(("parts", "blk", "sub", "rep"), None),
            P(("parts", "blk", "sub", "rep"), None),
        ),
        check_vma=False,
    )
```

profile of v0, /device:TPU:78, one launch (start us, length us, event | category | flops | bytes accessed | tf_op | source)
XLA Modules:
  0.0 134.1 jit_solution(3773919563160055687)
XLA Ops:
  0.7 0.7 reshape.67
  1.4 71.3 %all_gather.3 = bf16[64,32,128]{2,1,0:T(8,128)(2,1)S(1)} all-gather(bf16[4,32,128]{2,1,0:T(8,128)(2,1)} %param.7), channel_id=1, replica_groups=mesh['parts'=2,'blk'=16,'sub'=8,'rep'=2] {'blk'}, dimensions={0}, use_global_device_ids=true | all-gather | bytes 557056 | tf_op jit(solution)/shard_map/all_gather | solution.py:35
  72.6 31.6 %while.10 = (s32[]{:T(128)}, f32[16,64,4]{1,2,0:T(4,128)S(1)}, s32[16,4]{1,0:T(8,128)S(1)}, bf16[16,512,128]{2,1,0:T(8,128)(2,1)}, bf16[2048,128]{1,0:T(8,128)(2,1)S(1)}, /*index=5*/s32[]{:T(128)}, f32[]{:T(128)}) while((s32[]{:T(128)}, f32[16,64,4]{1,2,0:T(4,128)S(1)}, s32[16,4]{1,0:T(8,128)S(1)}, bf16[16,512,128]{2,1,0:T(8,128)(2,1)}, ...), condition=%wide.region_3.4_spmd, body=%wide.region_0.3_spmd.sunk | while | flops 270533120 | bytes 792725 | solution.py:30
  72.7 1.6 %select_reduce_fusion.2 = f32[2048,4]{0,1:T(4,128)S(1)} fusion(pred[4,128]{1,0:T(4,128)(4,1)S(1)} %iota_compare_fusion.2, bf16[2048,128]{1,0:T(8,128)(2,1)S(1)} %get-tuple-element.93, bf16[16,512,128]{2,1,0:T(8,128)(2,1)} %get-tuple-element.92, s32[]{:T(128)S(6)} %copy.19), kind=kOutput, calls=%fused_computation.2.clone.1 | convolution fusion | flops 270524416 | bytes 688644 | tf_op jit(solution)/shard_map/while/body/eval_jaxpr/dot_general | solution.py:22
  74.4 0.1 reshape.95
  74.5 0.1 reduce_sum.10
  74.7 1.6 %select_reduce_fusion.2 = f32[2048,4]{0,1:T(4,128)S(1)} fusion(pred[4,128]{1,0:T(4,128)(4,1)S(1)} %iota_compare_fusion.2, bf16[2048,128]{1,0:T(8,128)(2,1)S(1)} %get-tuple-element.93, bf16[16,512,128]{2,1,0:T(8,128)(2,1)} %get-tuple-element.92, s32[]{:T(128)S(6)} %copy.19), kind=kOutput, calls=%fused_computation.2.clone.1 | convolution fusion | flops 270524416 | bytes 688644 | tf_op jit(solution)/shard_map/while/body/eval_jaxpr/dot_general | solution.py:22
  76.5 0.1 reduce_sum.10
  76.7 1.6 %select_reduce_fusion.2 = f32[2048,4]{0,1:T(4,128)S(1)} fusion(pred[4,128]{1,0:T(4,128)(4,1)S(1)} %iota_compare_fusion.2, bf16[2048,128]{1,0:T(8,128)(2,1)S(1)} %get-tuple-element.93, bf16[16,512,128]{2,1,0:T(8,128)(2,1)} %get-tuple-element.92, s32[]{:T(128)S(6)} %copy.19), kind=kOutput, calls=%fused_computation.2.clone.1 | convolution fusion | flops 270524416 | bytes 688644 | tf_op jit(solution)/shard_map/while/body/eval_jaxpr/dot_general | solution.py:22
  78.3 0.1 reshape.95
  78.4 0.1 reduce_sum.10
  78.7 1.6 %select_reduce_fusion.2 = f32[2048,4]{0,1:T(4,128)S(1)} fusion(pred[4,128]{1,0:T(4,128)(4,1)S(1)} %iota_compare_fusion.2, bf16[2048,128]{1,0:T(8,128)(2,1)S(1)} %get-tuple-element.93, bf16[16,512,128]{2,1,0:T(8,128)(2,1)} %get-tuple-element.92, s32[]{:T(128)S(6)} %copy.19), kind=kOutput, calls=%fused_computation.2.clone.1 | convolution fusion | flops 270524416 | bytes 688644 | tf_op jit(solution)/shard_map/while/body/eval_jaxpr/dot_general | solution.py:22
  80.4 0.1 reduce_sum.10
  80.6 1.6 %select_reduce_fusion.2 = f32[2048,4]{0,1:T(4,128)S(1)} fusion(pred[4,128]{1,0:T(4,128)(4,1)S(1)} %iota_compare_fusion.2, bf16[2048,128]{1,0:T(8,128)(2,1)S(1)} %get-tuple-element.93, bf16[16,512,128]{2,1,0:T(8,128)(2,1)} %get-tuple-element.92, s32[]{:T(128)S(6)} %copy.19), kind=kOutput, calls=%fused_computation.2.clone.1 | convolution fusion | flops 270524416 | bytes 688644 | tf_op jit(solution)/shard_map/while/body/eval_jaxpr/dot_general | solution.py:22
  82.4 0.1 reduce_sum.10
  82.6 1.6 %select_reduce_fusion.2 = f32[2048,4]{0,1:T(4,128)S(1)} fusion(pred[4,128]{1,0:T(4,128)(4,1)S(1)} %iota_compare_fusion.2, bf16[2048,128]{1,0:T(8,128)(2,1)S(1)} %get-tuple-element.93, bf16[16,512,128]{2,1,0:T(8,128)(2,1)} %get-tuple-element.92, s32[]{:T(128)S(6)} %copy.19), kind=kOutput, calls=%fused_computation.2.clone.1 | convolution fusion | flops 270524416 | bytes 688644 | tf_op jit(solution)/shard_map/while/body/eval_jaxpr/dot_general | solution.py:22
  84.3 0.1 reshape.95
  84.4 0.1 reduce_sum.10
  84.6 1.6 %select_reduce_fusion.2 = f32[2048,4]{0,1:T(4,128)S(1)} fusion(pred[4,128]{1,0:T(4,128)(4,1)S(1)} %iota_compare_fusion.2, bf16[2048,128]{1,0:T(8,128)(2,1)S(1)} %get-tuple-element.93, bf16[16,512,128]{2,1,0:T(8,128)(2,1)} %get-tuple-element.92, s32[]{:T(128)S(6)} %copy.19), kind=kOutput, calls=%fused_computation.2.clone.1 | convolution fusion | flops 270524416 | bytes 688644 | tf_op jit(solution)/shard_map/while/body/eval_jaxpr/dot_general | solution.py:22
  86.3 0.1 reduce_sum.10
  86.6 1.6 %select_reduce_fusion.2 = f32[2048,4]{0,1:T(4,128)S(1)} fusion(pred[4,128]{1,0:T(4,128)(4,1)S(1)} %iota_compare_fusion.2, bf16[2048,128]{1,0:T(8,128)(2,1)S(1)} %get-tuple-element.93, bf16[16,512,128]{2,1,0:T(8,128)(2,1)} %get-tuple-element.92, s32[]{:T(128)S(6)} %copy.19), kind=kOutput, calls=%fused_computation.2.clone.1 | convolution fusion | flops 270524416 | bytes 688644 | tf_op jit(solution)/shard_map/while/body/eval_jaxpr/dot_general | solution.py:22
  88.3 0.1 reduce_sum.10
  88.6 1.6 %select_reduce_fusion.2 = f32[2048,4]{0,1:T(4,128)S(1)} fusion(pred[4,128]{1,0:T(4,128)(4,1)S(1)} %iota_compare_fusion.2, bf16[2048,128]{1,0:T(8,128)(2,1)S(1)} %get-tuple-element.93, bf16[16,512,128]{2,1,0:T(8,128)(2,1)} %get-tuple-element.92, s32[]{:T(128)S(6)} %copy.19), kind=kOutput, calls=%fused_computation.2.clone.1 | convolution fusion | flops 270524416 | bytes 688644 | tf_op jit(solution)/shard_map/while/body/eval_jaxpr/dot_general | solution.py:22
  90.3 0.1 reduce_sum.10
  90.5 1.6 %select_reduce_fusion.2 = f32[2048,4]{0,1:T(4,128)S(1)} fusion(pred[4,128]{1,0:T(4,128)(4,1)S(1)} %iota_compare_fusion.2, bf16[2048,128]{1,0:T(8,128)(2,1)S(1)} %get-tuple-element.93, bf16[16,512,128]{2,1,0:T(8,128)(2,1)} %get-tuple-element.92, s32[]{:T(128)S(6)} %copy.19), kind=kOutput, calls=%fused_computation.2.clone.1 | convolution fusion | flops 270524416 | bytes 688644 | tf_op jit(solution)/shard_map/while/body/eval_jaxpr/dot_general | solution.py:22
  92.3 0.1 reduce_sum.10
  92.5 1.6 %select_reduce_fusion.2 = f32[2048,4]{0,1:T(4,128)S(1)} fusion(pred[4,128]{1,0:T(4,128)(4,1)S(1)} %iota_compare_fusion.2, bf16[2048,128]{1,0:T(8,128)(2,1)S(1)} %get-tuple-element.93, bf16[16,512,128]{2,1,0:T(8,128)(2,1)} %get-tuple-element.92, s32[]{:T(128)S(6)} %copy.19), kind=kOutput, calls=%fused_computation.2.clone.1 | convolution fusion | flops 270524416 | bytes 688644 | tf_op jit(solution)/shard_map/while/body/eval_jaxpr/dot_general | solution.py:22
  94.3 0.1 reduce_sum.10
  94.5 1.6 %select_reduce_fusion.2 = f32[2048,4]{0,1:T(4,128)S(1)} fusion(pred[4,128]{1,0:T(4,128)(4,1)S(1)} %iota_compare_fusion.2, bf16[2048,128]{1,0:T(8,128)(2,1)S(1)} %get-tuple-element.93, bf16[16,512,128]{2,1,0:T(8,128)(2,1)} %get-tuple-element.92, s32[]{:T(128)S(6)} %copy.19), kind=kOutput, calls=%fused_computation.2.clone.1 | convolution fusion | flops 270524416 | bytes 688644 | tf_op jit(solution)/shard_map/while/body/eval_jaxpr/dot_general | solution.py:22
  96.2 0.1 reduce_sum.10
  96.5 1.6 %select_reduce_fusion.2 = f32[2048,4]{0,1:T(4,128)S(1)} fusion(pred[4,128]{1,0:T(4,128)(4,1)S(1)} %iota_compare_fusion.2, bf16[2048,128]{1,0:T(8,128)(2,1)S(1)} %get-tuple-element.93, bf16[16,512,128]{2,1,0:T(8,128)(2,1)} %get-tuple-element.92, s32[]{:T(128)S(6)} %copy.19), kind=kOutput, calls=%fused_computation.2.clone.1 | convolution fusion | flops 270524416 | bytes 688644 | tf_op jit(solution)/shard_map/while/body/eval_jaxpr/dot_general | solution.py:22
  98.2 0.1 reduce_sum.10
  98.5 1.6 %select_reduce_fusion.2 = f32[2048,4]{0,1:T(4,128)S(1)} fusion(pred[4,128]{1,0:T(4,128)(4,1)S(1)} %iota_compare_fusion.2, bf16[2048,128]{1,0:T(8,128)(2,1)S(1)} %get-tuple-element.93, bf16[16,512,128]{2,1,0:T(8,128)(2,1)} %get-tuple-element.92, s32[]{:T(128)S(6)} %copy.19), kind=kOutput, calls=%fused_computation.2.clone.1 | convolution fusion | flops 270524416 | bytes 688644 | tf_op jit(solution)/shard_map/while/body/eval_jaxpr/dot_general | solution.py:22
  100.2 0.1 reduce_sum.10
  100.4 1.6 %select_reduce_fusion.2 = f32[2048,4]{0,1:T(4,128)S(1)} fusion(pred[4,128]{1,0:T(4,128)(4,1)S(1)} %iota_compare_fusion.2, bf16[2048,128]{1,0:T(8,128)(2,1)S(1)} %get-tuple-element.93, bf16[16,512,128]{2,1,0:T(8,128)(2,1)} %get-tuple-element.92, s32[]{:T(128)S(6)} %copy.19), kind=kOutput, calls=%fused_computation.2.clone.1 | convolution fusion | flops 270524416 | bytes 688644 | tf_op jit(solution)/shard_map/while/body/eval_jaxpr/dot_general | solution.py:22
  102.2 0.1 reduce_sum.10
  102.4 1.6 %select_reduce_fusion.2 = f32[2048,4]{0,1:T(4,128)S(1)} fusion(pred[4,128]{1,0:T(4,128)(4,1)S(1)} %iota_compare_fusion.2, bf16[2048,128]{1,0:T(8,128)(2,1)S(1)} %get-tuple-element.93, bf16[16,512,128]{2,1,0:T(8,128)(2,1)} %get-tuple-element.92, s32[]{:T(128)S(6)} %copy.19), kind=kOutput, calls=%fused_computation.2.clone.1 | convolution fusion | flops 270524416 | bytes 688644 | tf_op jit(solution)/shard_map/while/body/eval_jaxpr/dot_general | solution.py:22
  104.2 0.1 reduce_sum.10
  104.3 0.3 reshape.91
  104.6 0.3 copy.13
  104.9 0.7 reshape.92
  105.6 3.9 %all-to-all-start = ((f32[16,1,256]{2,1,0:T(1,128)}), f32[16,1,256]{2,1,0:T(1,128)S(1)}, u32[]{:S(2)}, u32[]{:S(2)}) async-start(f32[16,1,256]{2,1,0:T(1,128)} %reshape.92), calls=%async_computation | async-start | bytes 32768 | tf_op jit(solution)/shard_map/all_to_all | solution.py:36
  109.6 4.5 %gather_fusion = s32[1024]{0:T(1024)S(1)} fusion(s32[1024]{0:T(1024)S(1)} %copy-done, s32[1024]{0:T(1024)S(1)} %broadcast_clamp_fusion), kind=kCustom, calls=%fused_computation | custom fusion | bytes 12288 | tf_op jit(solution)/shard_map/jit(_take)/gather | solution.py:37
  114.2 7.5 %all-to-all-done = f32[16,1,256]{2,1,0:T(1,128)S(1)} async-done(((f32[16,1,256]{2,1,0:T(1,128)}), f32[16,1,256]{2,1,0:T(1,128)S(1)}, u32[]{:S(2)}, u32[]{:S(2)}) %all-to-all-start) | async-done | bytes 16416 | tf_op jit(solution)/shard_map/all_to_all | solution.py:36
  121.6 0.5 broadcast.70
  122.1 0.7 reduce
  123.0 9.1 %gather_fusion.1 = f32[1024]{0:T(1024)S(1)} fusion(f32[4,1024]{1,0:T(4,128)S(1)} %all_to_all.17, s32[1024]{0:T(1024)S(1)} %bitcast.43), kind=kCustom, calls=%fused_computation.1 | custom fusion | bytes 16384 | tf_op jit(solution)/shard_map/jit(take_along_axis)/gather | solution.py:37
  132.2 1.9 %sort_prefixfusion = f32[4,10]{1,0:T(4,128)} fusion(f32[4,256]{1,0:T(4,128)S(1)} %and_select_fusion), kind=kCustom, calls=%top_k.9.sort_prefix | custom fusion | flops 10240 | bytes 4256 | tf_op jit(solution)/shard_map/top_k | solution.py:38
  (79 shorter events, 3.1 us)
Async XLA Ops:
  0.6 109.0 %copy-start = (s32[1024]{0:T(1024)S(1)}, s32[1024]{0:T(1024)}, u32[]{:S(2)}) copy-start(s32[1024]{0:T(1024)} %param.10) | copy-start | bytes 12292
  72.6 36.9 %copy-start.1 = (s32[4,256]{1,0:T(4,128)S(1)}, s32[4,256]{1,0:T(4,128)}, u32[]{:S(2)}) copy-start(s32[4,256]{1,0:T(4,128)} %param.11) | copy-start | bytes 12292
  105.6 16.0 %all-to-all-start = ((f32[16,1,256]{2,1,0:T(1,128)}), f32[16,1,256]{2,1,0:T(1,128)S(1)}, u32[]{:S(2)}, u32[]{:S(2)}) async-start(f32[16,1,256]{2,1,0:T(1,128)} %reshape.92), calls=%async_computation | async-start | bytes 32768 | tf_op jit(solution)/shard_map/all_to_all | solution.py:36
  132.2 1.9 %copy-start.2 = (f32[4,256]{1,0:T(4,128)}, f32[4,256]{1,0:T(4,128)S(1)}, u32[]{:S(2)}) copy-start(f32[4,256]{1,0:T(4,128)S(1)} %and_select_fusion) | copy-start | bytes 12292
where the time goes:
time: 135 us; the launch traced here: 134 us
  blocking collectives  71.3 us (53%)
  matrix products  26.2 us (19%)
  local copies, waits for them, and re-layouts  18.1 us (13%)
  waiting for transfers between devices  7.45 us (6%)
  other arithmetic  5.8 us (4%)
  starting transfers between devices  3.93 us (3%)
    all_gather x1, blocking collectives, shards(): lax.all_gather(queries, 'blk', axis=0, tiled=True)  71.3 us
    dot_general x16, matrix products, one_block(): lax.dot_general(flat, piece, (((1,), (1,)), ((), ())), preferred_element_...  26.2 us
    gather x2, local copies, waits for them, and re-layouts, shards(): jnp.take_along_axis(whole, jnp.take(slot_of, candidates, axis=0), axis=1)  9.13 us
    all_to_all x1, waiting for transfers between devices, shards(): lax.all_to_all(table, 'blk', split_axis=0, concat_axis=1, tiled=True)  7.45 us
    gather x2, local copies, waits for them, and re-layouts, shards(): jnp.take(slot_of, candidates, axis=0)  4.54 us
    all_to_all x1, starting transfers between devices, shards(): lax.all_to_all(table, 'blk', split_axis=0, concat_axis=1, tiled=True)  3.93 us
  transfers between devices with their start and end apart: 1, of which 1 were waited for; matrix products, arithmetic and copies ran while one was open for 3% of the time, Pallas kernels for 0%

commit v1 on v0

v1 whole, which is shorter than its diff:
```python
import functools

import jax
import jax.numpy as jnp
from jax import lax
from jax.experimental import pallas as pl
from jax.experimental.pallas import tpu as pltpu
from jax.sharding import PartitionSpec as P

MESH = pl.DeviceIdType.MESH
TOPN = 10
F32 = jnp.float32
BF16 = jnp.bfloat16


def slot(side, d):
    return 2 * d - 1 if side == 1 else 2 * d


def gather_rows(table, row_of, lane_of):
    found = jnp.zeros(row_of.shape, table.dtype)
    for row in range(table.shape[0]):
        line = jnp.broadcast_to(table[row : row + 1, :], row_of.shape)
        picked = jnp.take_along_axis(line, lane_of, axis=1, mode="promise_in_bounds")
        found = jnp.where(row_of == row, picked, found)
    return found


def kernel(
    n, q_ref, p_hbm, len_ref, slot_ref, cand_ref, score_ref, top_ref,
    own, held, stored, weights, best, outgoing, table, load_sem, send_sem, recv_sem, back_send, back_recv,
):
    me = lax.axis_index("blk")
    half = n // 2
    count, span, width = p_hbm.shape
    pairs = count // 2
    queries_here, tokens = q_ref.shape[0], q_ref.shape[1]
    cols = queries_here * tokens

    def at(shift):
        return {"blk": lax.rem(me + shift + n, n)}

    loads = []
    for side in range(2):
        load = pltpu.make_async_copy(
            p_hbm.at[pl.ds(side * pairs, pairs)],
            stored.at[:, :, pl.ds(side * width, width)],
            load_sem.at[side],
        )
        load.start()
        loads.append(load)

    barrier = pltpu.get_barrier_semaphore()
    for d in (4, 2, 1):
        for side in (1, -1):
            pl.semaphore_signal(barrier, inc=1, device_id=at(side * d), device_id_type=MESH)

    flat = q_ref[...].reshape(cols, width).astype(F32)
    own[...] = flat.T.astype(BF16)
    weights[...] = jnp.zeros_like(weights)

    pl.semaphore_wait(barrier, 6)

    started = []

    def send(side, hop, source, d):
        src = own if source == 0 else held.at[slot(side, source)]
        if d == half:
            part = pl.ds(0 if side == 1 else width // 2, width // 2)
            src = src.at[part]
            dst = held.at[n - 1].at[part]
            sem = n - 1 if side == 1 else n
        else:
            dst = held.at[slot(side, d)]
            sem = slot(side, d)
        copy = pltpu.make_async_remote_copy(
            src_ref=src, dst_ref=dst, send_sem=send_sem.at[sem], recv_sem=recv_sem.at[sem],
            device_id=at(side * hop), device_id_type=MESH,
        )
        copy.start()
        started.append(copy)

    def arrived(side, d):
        started_like[(side, d)].wait_recv()

    started_like = {}

    def send_both(hop, source, d):
        for side in (1, -1):
            send(side, hop, source, d)
            started_like[(side, d)] = started[-1]

    def wait_both(d):
        for side in (1, -1):
            arrived(side, d)

    send_both(4, 0, 4)
    send_both(2, 0, 2)
    send_both(1, 0, 1)

    cand = jnp.concatenate(
        [cand_ref[q : q + 1, h * 128 : (h + 1) * 128] for q in range(queries_here) for h in range(2)], axis=0
    )
    rows = gather_rows(slot_ref[...], cand // 128, cand % 128)
    query_of = lax.broadcasted_iota(jnp.int32, rows.shape, 0) // 2

    for load in loads:
        load.wait()

    def keep_live(pair, _):
        for side in range(2):
            lanes = pl.ds(side * width, width)
            piece = stored[pair, :, lanes].astype(F32)
            live = lax.broadcasted_iota(jnp.int32, piece.shape, 0) < len_ref[pair + side * pairs]
            stored[pair, :, lanes] = jnp.where(live, piece, piece[0:1, :]).astype(BF16)
        return 0

    lax.fori_loop(0, pairs, keep_live, 0)

    r_at = lax.broadcasted_iota(jnp.int32, (2 * cols, cols), 0) % cols
    c_at = lax.broadcasted_iota(jnp.int32, (2 * cols, cols), 1)
    ones_of = jnp.where(r_at // tokens == c_at // tokens, 1.0 / tokens, 0.0).astype(BF16)
    mine = (
        lax.broadcasted_iota(jnp.int32, (pairs, cols), 0) == lax.broadcasted_iota(jnp.int32, (pairs, cols), 1) % tokens
    )

    def score_block(query_cols):
        weights[0:width, 0:cols] = query_cols
        weights[width : 2 * width, cols : 2 * cols] = query_cols
        rhs = weights[...]
        for pair in range(pairs):
            similar = jnp.dot(stored[pair], rhs, preferred_element_type=F32)
            best[pair : pair + 1, :] = jnp.max(similar, axis=0, keepdims=True)
        lines = []
        for side in range(2):
            value = best[:, side * cols : (side + 1) * cols]
            high = value.astype(BF16)
            low = (value - high.astype(F32)).astype(BF16)
            summed = jnp.dot(jnp.concatenate([high, low], axis=1), ones_of, preferred_element_type=F32)
            lines.append(jnp.sum(jnp.where(mine, summed, 0.0), axis=0, keepdims=True))
        return jnp.concatenate(lines, axis=0)

    def back(s):
        d = (s + 1) // 2
        side = 2 * lax.rem(s, 2) - 1
        return pltpu.make_async_remote_copy(
            src_ref=outgoing.at[s], dst_ref=table.at[me], send_sem=back_send.at[s], recv_sem=back_recv.at[s],
            device_id=at(-side * d), device_id_type=MESH,
        )

    def score_slots(low, high):
        def one(s, _):
            outgoing[s] = score_block(held[s])
            back(s).start()
            return 0

        lax.fori_loop(low, high, one, 0)

    table[me] = score_block(own[...])

    wait_both(2)
    send_both(1, 2, 3)
    wait_both(1)
    score_slots(1, 3)
    wait_both(4)
    send_both(4, 4, 8)
    send_both(2, 4, 6)
    send_both(1, 4, 5)
    wait_both(3)
    score_slots(3, 7)
    wait_both(6)
    send_both(1, 6, 7)
    wait_both(5)
    score_slots(7, 13)
    wait_both(8)
    wait_both(7)
    score_slots(13, n)

    def land(s, _):
        back(s).wait_recv()
        return 0

    lax.fori_loop(1, n, land, 0)

    lines = table[...].reshape(2 * n, cols)
    score = gather_rows(lines, rows // tokens, query_of * tokens + rows % tokens)
    for q in range(queries_here):
        for h in range(2):
            score_ref[q : q + 1, h * 128 : (h + 1) * 128] = score[2 * q + h : 2 * q + h + 1, :]

    down = score.T
    j_at = lax.broadcasted_iota(jnp.int32, (128, 128), 0)
    k_at = lax.broadcasted_iota(jnp.int32, (128, 128), 1)
    place = lax.broadcasted_iota(jnp.int32, (16, 128), 0).astype(F32)
    spot = lax.broadcasted_iota(jnp.int32, (16, 128), 0) == lax.broadcasted_iota(jnp.int32, (16, 128), 1)
    for q in range(queries_here):
        total = jnp.zeros((16, 1), F32)
        for kh in range(2):
            k_val = score[2 * q + kh : 2 * q + kh + 1, :]
            rank = jnp.zeros((1, 128), F32)
            for jh in range(2):
                j_val = down[:, 2 * q + jh : 2 * q + jh + 1]
                if jh < kh:
                    ahead = j_val >= k_val
                elif jh > kh:
                    ahead = j_val > k_val
                else:
                    ahead = (j_val > k_val) | ((j_val == k_val) & (j_at < k_at))
                rank = rank + jnp.sum(jnp.where(ahead, 1.0, 0.0), axis=0, keepdims=True)
            total = total + jnp.sum(jnp.where(rank == place, k_val, 0.0), axis=1, keepdims=True)
        line = jnp.sum(jnp.where(spot, total, 0.0), axis=0, keepdims=True)
        top_ref[q : q + 1, :] = line[:, 0:TOPN]

    for copy in started:
        copy.wait_send()

    def sent(s, _):
        back(s).wait_send()
        return 0

    lax.fori_loop(1, n, sent, 0)


def shards(n, queries, passages, lengths, slot_of, candidates):
    queries_here, tokens, width = queries.shape
    count, span, _ = passages.shape
    cols = queries_here * tokens
    vmem = pl.BlockSpec(memory_space=pltpu.VMEM)
    return pl.pallas_call(
        functools.partial(kernel, n),
        out_shape=(
            jax.ShapeDtypeStruct(candidates.shape, F32),
            jax.ShapeDtypeStruct((queries_here, TOPN), F32),
        ),
        in_specs=[
            vmem,
            pl.BlockSpec(memory_space=pl.ANY),
            pl.BlockSpec(memory_space=pltpu.SMEM),
            vmem,
            vmem,
        ],
        out_specs=(vmem, vmem),
        scratch_shapes=[
            pltpu.VMEM((width, cols), BF16),
            pltpu.VMEM((n, width, cols), BF16),
            pltpu.VMEM((count // 2, span, 2 * width), BF16),
            pltpu.VMEM((2 * width, 2 * cols), BF16),
            pltpu.VMEM((count // 2, 2 * cols), F32),
            pltpu.VMEM((n, 2, cols), F32),
            pltpu.VMEM((n, 2, cols), F32),
            pltpu.SemaphoreType.DMA((2,)),
            pltpu.SemaphoreType.DMA((n + 1,)),
            pltpu.SemaphoreType.DMA((n + 1,)),
            pltpu.SemaphoreType.DMA((n,)),
            pltpu.SemaphoreType.DMA((n,)),
        ],
        compiler_params=pltpu.CompilerParams(collective_id=0, has_side_effects=True),
    )(queries, passages, lengths, slot_of.reshape(-1, 128), candidates)


def solution(mesh):
    return jax.shard_map(
        functools.partial(shards, mesh.shape["blk"]),
        mesh=mesh,
        in_specs=(
            P(("parts", "blk", "sub", "rep"), None, None),
            P(("parts", "blk"), None, None),
            P(("parts", "blk")),
            P("parts"),
            P(("parts", "blk", "sub", "rep"), None),
        ),
        out_specs=(
            P(("parts", "blk", "sub", "rep"), None),
            P(("parts", "blk", "sub", "rep"), None),
        ),
        check_vma=False,
    )
```

time: 135 us -> 76.8 us (0.57)
  Pallas kernels: 0 us -> 73.4 us
  blocking collectives: 71.3 us -> 0 us
  matrix products: 26.2 us -> 0 us
  local copies, waits for them, and re-layouts: 18.1 us -> 2.5 us
  waiting for transfers between devices: 7.45 us -> 0 us
  other arithmetic: 5.8 us -> 0 us
  starting transfers between devices: 3.93 us -> 0 us
    pallas_call x0 -> x1, Pallas kernels: none -> 73.4 us  [shards(): pl.pallas_call(functools.partial(kernel, n), out_shape=(jax.ShapeDtypeStr...]
    all_gather x1 -> x0, blocking collectives: 71.3 us -> none  [shards(): lax.all_gather(queries, 'blk', axis=0, tiled=True)]
    dot_general x16 -> x0, matrix products: 26.2 us -> none  [one_block(): lax.dot_general(flat, piece, (((1,), (1,)), ((), ())), preferred_element_...]
    gather x4 -> x0, local copies, waits for them, and re-layouts: 13.7 us -> none  [the longest x2 9.13 us: shards(): jnp.take_along_axis(whole, jnp.take(slot_of, candidates, axis=0), axis=1)]
    all_to_all x1 -> x0, waiting for transfers between devices: 7.45 us -> none  [shards(): lax.all_to_all(table, 'blk', split_axis=0, concat_axis=1, tiled=True)]
    all_to_all x1 -> x0, starting transfers between devices: 3.93 us -> none  [shards(): lax.all_to_all(table, 'blk', split_axis=0, concat_axis=1, tiled=True)]
    reshape x17 -> x0, local copies, waits for them, and re-layouts: 2.32 us -> none  [the longest x16 1.58 us: one_block(): return jnp.sum(best.reshape(queries_here, tokens, group), axis=1) / tokens]
    top_k x1 -> x0, other arithmetic: 1.93 us -> none  [shards(): top = lax.top_k(score, TOPN)[0]]
  transfers between devices with their start and end apart: 1 -> 0, of which waited for: 1 -> 0; matrix products, arithmetic and copies ran while one was open for 3% -> 0% of each run, Pallas kernels for 0% -> 0%
where the time goes in v1:
time: 76.8 us; the launch traced here: 76.5 us
  Pallas kernels  73.4 us (96%)
  local copies, waits for them, and re-layouts  2.5 us (3%)
    pallas_call x1, Pallas kernels, shards(): pl.pallas_call(functools.partial(kernel, n), out_shape=(jax.ShapeDtypeStr...  73.4 us
    unnamed x2, local copies, waits for them, and re-layouts  2.5 us

profile of v1, /device:TPU:78, one launch (start us, length us, event | category | flops | bytes accessed | tf_op | source)
XLA Modules:
  0.0 76.5 jit_solution(2166117506015447394)
XLA Ops:
  0.6 73.4 %shard_map.68 = (f32[4,256]{1,0:T(4,128)}, f32[4,10]{1,0:T(4,128)}) custom-call(bf16[4,32,128]{2,1,0:T(8,128)(2,1)} %q_ref.1, bf16[64,128,128]{2,1,0:T(8,128)(2,1)} %p_hbm.1, s32[64]{0:T(128)} %len_ref.1, s32[8,128]{1,0:T(8,128)} %bitcast.1, s32[4,256]{1,0:T(4,128)} %cand_ref.1), custom_call_target="tpu_custom_call" | custom-call | tf_op jit(solution)/shard_map/pallas_call | solution.py:229
  74.0 1.3 %copy.9 = f32[4,256]{1,0:T(4,128)} copy(f32[4,256]{1,0:T(4,128)} %get-tuple-element.4) | data formatting | bytes 8192
  75.3 1.2 %copy.10 = f32[4,10]{1,0:T(4,128)} copy(f32[4,10]{1,0:T(4,128)} %get-tuple-element.5) | data formatting | bytes 320

commit v2 on v1

--- a/solution.py
+++ b/solution.py
@@ -11,10 +11,6 @@
 TOPN = 10
 F32 = jnp.float32
 BF16 = jnp.bfloat16
-
-
-def slot(side, d):
-    return 2 * d - 1 if side == 1 else 2 * d
 
 
 def gather_rows(table, row_of, lane_of):
@@ -28,17 +24,15 @@
 
 def kernel(
     n, q_ref, p_hbm, len_ref, slot_ref, cand_ref, score_ref, top_ref,
-    own, held, stored, weights, best, outgoing, table, load_sem, send_sem, recv_sem, back_send, back_recv,
+    own, held, stored, weights, best, outgoing, table, load_sem, up_send, down_send, recv_sem, back_send, back_recv,
 ):
     me = lax.axis_index("blk")
-    half = n // 2
     count, span, width = p_hbm.shape
     pairs = count // 2
     queries_here, tokens = q_ref.shape[0], q_ref.shape[1]
     cols = queries_here * tokens
 
-    def at(shift):
-        return {"blk": lax.rem(me + shift + n, n)}
+    last = n - 1
 
     loads = []
     for side in range(2):
@@ -51,52 +45,36 @@
         loads.append(load)
 
     barrier = pltpu.get_barrier_semaphore()
-    for d in (4, 2, 1):
-        for side in (1, -1):
-            pl.semaphore_signal(barrier, inc=1, device_id=at(side * d), device_id_type=MESH)
+    pl.semaphore_signal(barrier, inc=1, device_id={"blk": lax.rem(me + last, n)}, device_id_type=MESH)
 
     flat = q_ref[...].reshape(cols, width).astype(F32)
     own[...] = flat.T.astype(BF16)
     weights[...] = jnp.zeros_like(weights)
 
-    pl.semaphore_wait(barrier, 6)
-
-    started = []
-
-    def send(side, hop, source, d):
-        src = own if source == 0 else held.at[slot(side, source)]
-        if d == half:
-            part = pl.ds(0 if side == 1 else width // 2, width // 2)
-            src = src.at[part]
-            dst = held.at[n - 1].at[part]
-            sem = n - 1 if side == 1 else n
-        else:
-            dst = held.at[slot(side, d)]
-            sem = slot(side, d)
-        copy = pltpu.make_async_remote_copy(
-            src_ref=src, dst_ref=dst, send_sem=send_sem.at[sem], recv_sem=recv_sem.at[sem],
-            device_id=at(side * hop), device_id_type=MESH,
-        )
-        copy.start()
-        started.append(copy)
-
-    def arrived(side, d):
-        started_like[(side, d)].wait_recv()
-
-    started_like = {}
-
-    def send_both(hop, source, d):
-        for side in (1, -1):
-            send(side, hop, source, d)
-            started_like[(side, d)] = started[-1]
-
-    def wait_both(d):
-        for side in (1, -1):
-            arrived(side, d)
-
-    send_both(4, 0, 4)
-    send_both(2, 0, 2)
-    send_both(1, 0, 1)
+    def climb(k, src):
+        return pltpu.make_async_remote_copy(
+            src_ref=src, dst_ref=held.at[k], send_sem=up_send.at[k], recv_sem=recv_sem.at[k],
+            device_id={"blk": lax.rem(me + 1, n)}, device_id_type=MESH,
+        )
+
+    def direct(k):
+        return pltpu.make_async_remote_copy(
+            src_ref=own, dst_ref=held.at[me], send_sem=down_send.at[k], recv_sem=recv_sem.at[me],
+            device_id={"blk": k}, device_id_type=MESH,
+        )
+
+    def back(k):
+        return pltpu.make_async_remote_copy(
+            src_ref=outgoing.at[k], dst_ref=table.at[me], send_sem=back_send.at[k], recv_sem=back_recv.at[me],
+            device_id={"blk": k}, device_id_type=MESH,
+        )
+
+    def loop(low, high, step):
+        def one(k, _):
+            step(k)
+            return 0
+
+        lax.fori_loop(low, high, one, 0)
 
     cand = jnp.concatenate(
         [cand_ref[q : q + 1, h * 128 : (h + 1) * 128] for q in range(queries_here) for h in range(2)], axis=0
@@ -140,47 +118,49 @@
             lines.append(jnp.sum(jnp.where(mine, summed, 0.0), axis=0, keepdims=True))
         return jnp.concatenate(lines, axis=0)
 
-    def back(s):
-        d = (s + 1) // 2
-        side = 2 * lax.rem(s, 2) - 1
-        return pltpu.make_async_remote_copy(
-            src_ref=outgoing.at[s], dst_ref=table.at[me], send_sem=back_send.at[s], recv_sem=back_recv.at[s],
-            device_id=at(-side * d), device_id_type=MESH,
-        )
-
-    def score_slots(low, high):
-        def one(s, _):
-            outgoing[s] = score_block(held[s])
-            back(s).start()
-            return 0
-
-        lax.fori_loop(low, high, one, 0)
+    def arrived(k):
+        pltpu.make_async_remote_copy(
+            src_ref=own, dst_ref=held.at[k], send_sem=up_send.at[k], recv_sem=recv_sem.at[k],
+            device_id={"blk": me}, device_id_type=MESH,
+        ).wait_recv()
+
+    def landed(k):
+        pltpu.make_async_remote_copy(
+            src_ref=outgoing.at[k], dst_ref=table.at[k], send_sem=back_send.at[k], recv_sem=back_recv.at[k],
+            device_id={"blk": me}, device_id_type=MESH,
+        ).wait_recv()
 
     table[me] = score_block(own[...])
 
-    wait_both(2)
-    send_both(1, 2, 3)
-    wait_both(1)
-    score_slots(1, 3)
-    wait_both(4)
-    send_both(4, 4, 8)
-    send_both(2, 4, 6)
-    send_both(1, 4, 5)
-    wait_both(3)
-    score_slots(3, 7)
-    wait_both(6)
-    send_both(1, 6, 7)
-    wait_both(5)
-    score_slots(7, 13)
-    wait_both(8)
-    wait_both(7)
-    score_slots(13, n)
-
-    def land(s, _):
-        back(s).wait_recv()
-        return 0
-
-    lax.fori_loop(1, n, land, 0)
+    pl.semaphore_wait(barrier, 1)
+
+    def answer(k):
+        outgoing[k] = score_block(held[k])
+        back(k).start()
+
+    def from_below(k):
+        arrived(k)
+
+        @pl.when(me < last)
+        def _():
+            climb(k, held.at[k]).start()
+
+        answer(k)
+
+    def from_above(k):
+        arrived(k)
+        answer(k)
+
+    loop(0, me, from_below)
+
+    @pl.when(me < last)
+    def _():
+        climb(me, own).start()
+
+    loop(0, me, lambda k: direct(k).start())
+    loop(me + 1, n, from_above)
+    loop(0, me, landed)
+    loop(me + 1, n, landed)
 
     lines = table[...].reshape(2 * n, cols)
     score = gather_rows(lines, rows // tokens, query_of * tokens + rows % tokens)
@@ -211,14 +191,14 @@
         line = jnp.sum(jnp.where(spot, total, 0.0), axis=0, keepdims=True)
         top_ref[q : q + 1, :] = line[:, 0:TOPN]
 
-    for copy in started:
-        copy.wait_send()
-
-    def sent(s, _):
-        back(s).wait_send()
-        return 0
-
-    lax.fori_loop(1, n, sent, 0)
+    @pl.when(me < last)
+    def _():
+        loop(0, me, lambda k: climb(k, held.at[k]).wait_send())
+        climb(me, own).wait_send()
+
+    loop(0, me, lambda k: direct(k).wait_send())
+    loop(0, me, lambda k: back(k).wait_send())
+    loop(me + 1, n, lambda k: back(k).wait_send())
 
 
 def shards(n, queries, passages, lengths, slot_of, candidates):
@@ -249,8 +229,9 @@
             pltpu.VMEM((n, 2, cols), F32),
             pltpu.VMEM((n, 2, cols), F32),
             pltpu.SemaphoreType.DMA((2,)),
-            pltpu.SemaphoreType.DMA((n + 1,)),
-            pltpu.SemaphoreType.DMA((n + 1,)),
+            pltpu.SemaphoreType.DMA((n,)),
+            pltpu.SemaphoreType.DMA((n,)),
+            pltpu.SemaphoreType.DMA((n,)),
             pltpu.SemaphoreType.DMA((n,)),
             pltpu.SemaphoreType.DMA((n,)),
         ],

time: 76.8 us -> 116 us (1.51)
  the two profiles are of different devices: /device:TPU:78 before, /device:TPU:320 now
where the time goes in v2:
time: 116 us
  Pallas kernels  113 us (97%)
  local copies, waits for them, and re-layouts  2.5 us (2%)
    pallas_call x1, Pallas kernels, shards(): pl.pallas_call(functools.partial(kernel, n), out_shape=(jax.ShapeDtypeStr...  113 us
    unnamed x2, local copies, waits for them, and re-layouts  2.5 us

profile of v2, /device:TPU:320, one launch (start us, length us, event | category | flops | bytes accessed | tf_op | source)
XLA Modules:
  0.0 116.1 jit_solution(786124315177058837)
XLA Ops:
  0.6 113.0 %shard_map.68 = (f32[4,256]{1,0:T(4,128)}, f32[4,10]{1,0:T(4,128)}) custom-call(bf16[4,32,128]{2,1,0:T(8,128)(2,1)} %q_ref.1, bf16[64,128,128]{2,1,0:T(8,128)(2,1)} %p_hbm.1, s32[64]{0:T(128)} %len_ref.1, s32[8,128]{1,0:T(8,128)} %bitcast.1, s32[4,256]{1,0:T(4,128)} %cand_ref.1), custom_call_target="tpu_custom_call" | custom-call | tf_op jit(solution)/shard_map/pallas_call | solution.py:209
  113.6 1.3 %copy.9 = f32[4,256]{1,0:T(4,128)} copy(f32[4,256]{1,0:T(4,128)} %get-tuple-element.4) | data formatting | bytes 8192
  114.9 1.2 %copy.10 = f32[4,10]{1,0:T(4,128)} copy(f32[4,10]{1,0:T(4,128)} %get-tuple-element.5) | data formatting | bytes 320

commit v3 on v2

--- a/solution.py
+++ b/solution.py
@@ -9,8 +9,43 @@
 
 MESH = pl.DeviceIdType.MESH
 TOPN = 10
+HOT = 4
 F32 = jnp.float32
 BF16 = jnp.bfloat16
+
+
+def order(z, n, hot):
+    last = n - 1
+    if z == 0:
+        return list(range(1, n))
+    if z < hot:
+        rest = [k for k in range(1, n) if k != z]
+        return rest[:9] + [0] + rest[9:]
+    sources = list(range(hot, z))
+    if z > n // 2:
+        for k in range(hot):
+            sources.insert(min(1 + 2 * (k + last - z), len(sources)), k)
+        return sources + list(range(z + 1, n))
+    sources += list(range(1, hot)) + list(range(z + 1, n))
+    return sources[:9] + [0] + sources[9:]
+
+
+def picked_by(table, me):
+    words = []
+    for start in range(0, len(table[0]), 5):
+        word = jnp.int32(0)
+        for z, line in enumerate(table):
+            packed = sum(value * 32**i for i, value in enumerate(line[start : start + 5]))
+            word = jnp.where(me == z, packed, word)
+        words.append(word)
+
+    def pick(at):
+        word = words[-1]
+        for i in range(len(words) - 1):
+            word = jnp.where(at // 5 == i, words[i], word)
+        return lax.rem(lax.shift_right_logical(word, 5 * lax.rem(at, 5)), 32)
+
+    return pick
 
 
 def gather_rows(table, row_of, lane_of):
@@ -24,7 +59,7 @@
 
 def kernel(
     n, q_ref, p_hbm, len_ref, slot_ref, cand_ref, score_ref, top_ref,
-    own, held, stored, weights, best, outgoing, table, load_sem, up_send, down_send, recv_sem, back_send, back_recv,
+    own, held, stored, weights, best, outgoing, table, load_sem, up_send, down_send, recv_sem, back_send, back_recv, asked,
 ):
     me = lax.axis_index("blk")
     count, span, width = p_hbm.shape
@@ -33,6 +68,8 @@
     cols = queries_here * tokens
 
     last = n - 1
+    hot = HOT
+    lag = n // 2
 
     loads = []
     for side in range(2):
@@ -44,9 +81,6 @@
         load.start()
         loads.append(load)
 
-    barrier = pltpu.get_barrier_semaphore()
-    pl.semaphore_signal(barrier, inc=1, device_id={"blk": lax.rem(me + last, n)}, device_id_type=MESH)
-
     flat = q_ref[...].reshape(cols, width).astype(F32)
     own[...] = flat.T.astype(BF16)
     weights[...] = jnp.zeros_like(weights)
@@ -75,6 +109,29 @@
             return 0
 
         lax.fori_loop(low, high, one, 0)
+
+    barrier = pltpu.get_barrier_semaphore()
+
+    @pl.when(me > 1)
+    def _():
+        pl.semaphore_wait(barrier, 1)
+
+    @pl.when(me > 0)
+    def _():
+        pl.semaphore_signal(barrier, inc=1, device_id={"blk": 0}, device_id_type=MESH)
+
+    @pl.when((me > 0) & (me < last))
+    def _():
+        pl.semaphore_signal(barrier, inc=1, device_id={"blk": lax.rem(me + 1, n)}, device_id_type=MESH)
+
+    def ask(k):
+        pl.semaphore_signal(asked.at[me], inc=1, device_id={"blk": k}, device_id_type=MESH)
+
+    @pl.when(me > hot)
+    def _():
+        ask(lax.rem(me + last, n))
+
+    loop(1, jnp.minimum(me, hot), ask)
 
     cand = jnp.concatenate(
         [cand_ref[q : q + 1, h * 128 : (h + 1) * 128] for q in range(queries_here) for h in range(2)], axis=0
@@ -132,33 +189,76 @@
 
     table[me] = score_block(own[...])
 
-    pl.semaphore_wait(barrier, 1)
+    source_at = picked_by([order(z, n, hot) for z in range(n)], me)
 
     def answer(k):
         outgoing[k] = score_block(held[k])
         back(k).start()
 
-    def from_below(k):
-        arrived(k)
-
-        @pl.when(me < last)
-        def _():
-            climb(k, held.at[k]).start()
-
-        answer(k)
-
-    def from_above(k):
-        arrived(k)
-        answer(k)
-
-    loop(0, me, from_below)
-
-    @pl.when(me < last)
-    def _():
-        climb(me, own).start()
-
-    loop(0, me, lambda k: direct(k).start())
-    loop(me + 1, n, from_above)
+    @pl.when(me < hot)
+    def _():
+        loop(1, me, lambda k: direct(k).start())
+
+        def step(t):
+            later = me + 1 + t
+
+            @pl.when(later < n)
+            def _():
+                @pl.when(me == 0)
+                def _():
+                    pl.semaphore_wait(barrier, 1)
+
+                @pl.when(me > 0)
+                def _():
+                    pl.semaphore_wait(asked.at[later], 1)
+
+                direct(later).start()
+
+            @pl.when(t >= lag)
+            def _():
+                k = source_at(jnp.maximum(t - lag, 0))
+                arrived(k)
+
+                @pl.when(k == 0)
+                def _():
+                    direct(k).start()
+
+                answer(k)
+
+        loop(0, last + lag, step)
+
+    @pl.when(me >= hot)
+    def _():
+        def step(t):
+            k = source_at(t)
+            arrived(k)
+
+            @pl.when(k == 0)
+            def _():
+                direct(k).start()
+
+            @pl.when(me < last)
+            def _():
+                @pl.when(t == 0)
+                def _():
+                    pl.semaphore_wait(asked.at[lax.rem(me + 1, n)], 1)
+
+                @pl.when((k >= hot) & (k < me))
+                def _():
+                    climb(k, held.at[k]).start()
+
+                @pl.when(t == 0)
+                def _():
+                    climb(me, own).start()
+
+            answer(k)
+
+            @pl.when(t < me - 1)
+            def _():
+                direct(jnp.where(lax.rem(t, 2) == 0, 1 + t // 2, me - 1 - t // 2)).start()
+
+        loop(0, last, step)
+
     loop(0, me, landed)
     loop(me + 1, n, landed)
 
@@ -191,14 +291,23 @@
         line = jnp.sum(jnp.where(spot, total, 0.0), axis=0, keepdims=True)
         top_ref[q : q + 1, :] = line[:, 0:TOPN]
 
-    @pl.when(me < last)
-    def _():
-        loop(0, me, lambda k: climb(k, held.at[k]).wait_send())
+    @pl.when((me >= hot) & (me < last))
+    def _():
+        loop(hot, me, lambda k: climb(k, held.at[k]).wait_send())
         climb(me, own).wait_send()
 
-    loop(0, me, lambda k: direct(k).wait_send())
+    @pl.when(me < hot)
+    def _():
+        loop(me + 1, n, lambda k: direct(k).wait_send())
+
     loop(0, me, lambda k: back(k).wait_send())
     loop(me + 1, n, lambda k: back(k).wait_send())
+
+    @pl.when(me > 0)
+    def _():
+        direct(jnp.int32(0)).wait_send()
+
+    loop(1, me, lambda k: direct(k).wait_send())
 
 
 def shards(n, queries, passages, lengths, slot_of, candidates):
@@ -234,6 +343,7 @@
             pltpu.SemaphoreType.DMA((n,)),
             pltpu.SemaphoreType.DMA((n,)),
             pltpu.SemaphoreType.DMA((n,)),
+            pltpu.SemaphoreType.REGULAR((n,)),
         ],
         compiler_params=pltpu.CompilerParams(collective_id=0, has_side_effects=True),
     )(queries, passages, lengths, slot_of.reshape(-1, 128), candidates)

time: 116 us -> 97.3 us (0.84)
  the two profiles are of different devices: /device:TPU:320 before, /device:TPU:78 now
where the time goes in v3:
time: 97.3 us; the launch traced here: 96.9 us
  Pallas kernels  93.8 us (96%)
  local copies, waits for them, and re-layouts  2.5 us (3%)
    pallas_call x1, Pallas kernels, shards(): pl.pallas_call(functools.partial(kernel, n), out_shape=(jax.ShapeDtypeStr...  93.8 us
    unnamed x2, local copies, waits for them, and re-layouts  2.5 us

profile of v3, /device:TPU:78, one launch (start us, length us, event | category | flops | bytes accessed | tf_op | source)
XLA Modules:
  0.0 96.9 jit_solution(5377742404054357094)
XLA Ops:
  0.6 93.8 %shard_map.68 = (f32[4,256]{1,0:T(4,128)}, f32[4,10]{1,0:T(4,128)}) custom-call(bf16[4,32,128]{2,1,0:T(8,128)(2,1)} %q_ref.1, bf16[64,128,128]{2,1,0:T(8,128)(2,1)} %p_hbm.1, s32[64]{0:T(128)} %len_ref.1, s32[8,128]{1,0:T(8,128)} %bitcast.1, s32[4,256]{1,0:T(4,128)} %cand_ref.1), custom_call_target="tpu_custom_call" | custom-call | tf_op jit(solution)/shard_map/pallas_call | solution.py:318
  94.4 1.3 %copy.9 = f32[4,256]{1,0:T(4,128)} copy(f32[4,256]{1,0:T(4,128)} %get-tuple-element.4) | data formatting | bytes 8192
  95.7 1.2 %copy.10 = f32[4,10]{1,0:T(4,128)} copy(f32[4,10]{1,0:T(4,128)} %get-tuple-element.5) | data formatting | bytes 320

commit v4 on v2

--- a/solution.py
+++ b/solution.py
@@ -9,8 +9,46 @@
 
 MESH = pl.DeviceIdType.MESH
 TOPN = 10
+REACH = 4
+LAG = 15
+ORDER = [
+    [1, 2, 3, 4, 5, 15, 6, 7, 11, 9, 8, 13, 12, 10, 14],
+    [3, 7, 9, 8, 6, 4, 5, 10, 12, 11, 13, 0, 14, 15, 2],
+    [1, 4, 7, 6, 9, 8, 3, 10, 5, 0, 11, 12, 13, 14, 15],
+    [1, 2, 9, 6, 8, 0, 5, 4, 10, 11, 13, 12, 14, 7, 15],
+    [1, 2, 3, 0, 8, 9, 5, 7, 10, 11, 6, 12, 13, 14, 15],
+    [1, 2, 3, 4, 7, 0, 8, 6, 9, 10, 11, 12, 13, 14, 15],
+    [1, 2, 3, 4, 5, 0, 9, 8, 10, 7, 11, 12, 13, 14, 15],
+    [1, 2, 3, 4, 5, 8, 6, 0, 9, 10, 11, 13, 14, 15, 12],
+    [1, 2, 3, 5, 4, 9, 6, 7, 0, 11, 10, 12, 13, 14, 15],
+    [1, 2, 3, 8, 5, 4, 6, 7, 0, 13, 11, 10, 12, 14, 15],
+    [1, 2, 3, 4, 5, 12, 6, 7, 11, 0, 8, 9, 13, 14, 15],
+    [1, 2, 3, 13, 4, 5, 0, 6, 7, 12, 10, 8, 9, 14, 15],
+    [1, 2, 3, 4, 5, 0, 6, 7, 10, 8, 9, 11, 14, 13, 15],
+    [1, 2, 3, 0, 4, 14, 5, 6, 7, 12, 8, 9, 11, 15, 10],
+    [1, 2, 0, 3, 4, 5, 6, 7, 12, 8, 9, 11, 13, 10, 15],
+    [0, 1, 2, 3, 4, 5, 6, 7, 8, 9, 11, 10, 12, 13, 14],
+]
 F32 = jnp.float32
 BF16 = jnp.bfloat16
+
+
+def picked_by(table, me):
+    words = []
+    for start in range(0, len(table[0]), 5):
+        word = jnp.int32(0)
+        for z, line in enumerate(table):
+            packed = sum(value * 32**i for i, value in enumerate(line[start : start + 5]))
+            word = jnp.where(me == z, packed, word)
+        words.append(word)
+
+    def pick(at):
+        word = words[-1]
+        for i in range(len(words) - 1):
+            word = jnp.where(at // 5 == i, words[i], word)
+        return lax.rem(lax.shift_right_logical(word, 5 * lax.rem(at, 5)), 32)
+
+    return pick
 
 
 def gather_rows(table, row_of, lane_of):
@@ -24,7 +62,7 @@
 
 def kernel(
     n, q_ref, p_hbm, len_ref, slot_ref, cand_ref, score_ref, top_ref,
-    own, held, stored, weights, best, outgoing, table, load_sem, up_send, down_send, recv_sem, back_send, back_recv,
+    own, held, stored, weights, best, outgoing, table, load_sem, up_send, down_send, recv_sem, back_send, back_recv, here,
 ):
     me = lax.axis_index("blk")
     count, span, width = p_hbm.shape
@@ -44,9 +82,6 @@
         load.start()
         loads.append(load)
 
-    barrier = pltpu.get_barrier_semaphore()
-    pl.semaphore_signal(barrier, inc=1, device_id={"blk": lax.rem(me + last, n)}, device_id_type=MESH)
-
     flat = q_ref[...].reshape(cols, width).astype(F32)
     own[...] = flat.T.astype(BF16)
     weights[...] = jnp.zeros_like(weights)
@@ -75,6 +110,34 @@
             return 0
 
         lax.fori_loop(low, high, one, 0)
+
+    barrier = pltpu.get_barrier_semaphore()
+
+    @pl.when(me > 1)
+    def _():
+        pl.semaphore_wait(barrier, 1)
+
+    @pl.when(me > 0)
+    def _():
+        pl.semaphore_signal(barrier, inc=1, device_id={"blk": 0}, device_id_type=MESH)
+
+    @pl.when((me > 0) & (me < last))
+    def _():
+        pl.semaphore_signal(barrier, inc=1, device_id={"blk": lax.rem(me + 1, n)}, device_id_type=MESH)
+
+    @pl.when(me > 1)
+    def _():
+        pl.semaphore_signal(here, inc=1, device_id={"blk": lax.rem(me + last, n)}, device_id_type=MESH)
+
+    near = jnp.maximum(1, me - REACH)
+
+    @pl.when(me > 0)
+    def _():
+        @pl.when(me - 1 > REACH)
+        def _():
+            direct(jnp.int32(1)).start()
+
+        loop(near, me, lambda k: direct(k).start())
 
     cand = jnp.concatenate(
         [cand_ref[q : q + 1, h * 128 : (h + 1) * 128] for q in range(queries_here) for h in range(2)], axis=0
@@ -132,33 +195,59 @@
 
     table[me] = score_block(own[...])
 
-    pl.semaphore_wait(barrier, 1)
+    source_at = picked_by(ORDER, me)
 
     def answer(k):
         outgoing[k] = score_block(held[k])
         back(k).start()
 
-    def from_below(k):
-        arrived(k)
-
-        @pl.when(me < last)
-        def _():
-            climb(k, held.at[k]).start()
-
-        answer(k)
-
-    def from_above(k):
-        arrived(k)
-        answer(k)
-
-    loop(0, me, from_below)
-
-    @pl.when(me < last)
-    def _():
+    @pl.when(me == 0)
+    def _():
+        def step(t):
+            @pl.when(t < last)
+            def _():
+                pl.semaphore_wait(barrier, 1)
+                direct(t + 1).start()
+
+            @pl.when(t >= LAG)
+            def _():
+                k = source_at(jnp.maximum(t - LAG, 0))
+                arrived(k)
+                answer(k)
+
+        loop(0, last + LAG, step)
+
+    @pl.when(me == 1)
+    def _():
+        pl.semaphore_wait(here, 1)
         climb(me, own).start()
 
-    loop(0, me, lambda k: direct(k).start())
-    loop(me + 1, n, from_above)
+    @pl.when(me > 0)
+    def _():
+        def step(t):
+            k = source_at(t)
+            arrived(k)
+
+            @pl.when(k == 0)
+            def _():
+                direct(k).start()
+
+            @pl.when((t == 0) & (me > 1) & (me < last))
+            def _():
+                pl.semaphore_wait(here, 1)
+
+            @pl.when(((k > 0) & (k < me) & (me < last)) | (k - me > REACH + 1))
+            def _():
+                climb(k, held.at[k]).start()
+
+            @pl.when((t == 0) & (me > 1) & (me < last))
+            def _():
+                climb(me, own).start()
+
+            answer(k)
+
+        loop(0, last, step)
+
     loop(0, me, landed)
     loop(me + 1, n, landed)
 
@@ -191,12 +280,26 @@
         line = jnp.sum(jnp.where(spot, total, 0.0), axis=0, keepdims=True)
         top_ref[q : q + 1, :] = line[:, 0:TOPN]
 
-    @pl.when(me < last)
-    def _():
-        loop(0, me, lambda k: climb(k, held.at[k]).wait_send())
+    @pl.when((me > 0) & (me < last))
+    def _():
+        loop(1, me, lambda k: climb(k, held.at[k]).wait_send())
         climb(me, own).wait_send()
-
-    loop(0, me, lambda k: direct(k).wait_send())
+        loop(me + REACH + 2, n, lambda k: climb(k, held.at[k]).wait_send())
+
+    @pl.when(me == 0)
+    def _():
+        loop(1, n, lambda k: direct(k).wait_send())
+
+    @pl.when(me > 0)
+    def _():
+        direct(jnp.int32(0)).wait_send()
+
+        @pl.when(me - 1 > REACH)
+        def _():
+            direct(jnp.int32(1)).wait_send()
+
+        loop(near, me, lambda k: direct(k).wait_send())
+
     loop(0, me, lambda k: back(k).wait_send())
     loop(me + 1, n, lambda k: back(k).wait_send())
 
@@ -234,6 +337,7 @@
             pltpu.SemaphoreType.DMA((n,)),
             pltpu.SemaphoreType.DMA((n,)),
             pltpu.SemaphoreType.DMA((n,)),
+            pltpu.SemaphoreType.REGULAR,
         ],
         compiler_params=pltpu.CompilerParams(collective_id=0, has_side_effects=True),
     )(queries, passages, lengths, slot_of.reshape(-1, 128), candidates)

time: 116 us -> 69.5 us (0.60)
  the two profiles are of different devices: /device:TPU:320 before, /device:TPU:78 now
where the time goes in v4:
time: 69.5 us; the launch traced here: 69.2 us
  Pallas kernels  66 us (95%)
  local copies, waits for them, and re-layouts  2.5 us (4%)
    pallas_call x1, Pallas kernels, shards(): pl.pallas_call(functools.partial(kernel, n), out_shape=(jax.ShapeDtypeStr...  66 us
    unnamed x2, local copies, waits for them, and re-layouts  2.5 us

profile of v4, /device:TPU:78, one launch (start us, length us, event | category | flops | bytes accessed | tf_op | source)
XLA Modules:
  0.0 69.2 jit_solution(1607851922292610164)
XLA Ops:
  0.6 66.0 %shard_map.68 = (f32[4,256]{1,0:T(4,128)}, f32[4,10]{1,0:T(4,128)}) custom-call(bf16[4,32,128]{2,1,0:T(8,128)(2,1)} %q_ref.1, bf16[64,128,128]{2,1,0:T(8,128)(2,1)} %p_hbm.1, s32[64]{0:T(128)} %len_ref.1, s32[8,128]{1,0:T(8,128)} %bitcast.1, s32[4,256]{1,0:T(4,128)} %cand_ref.1), custom_call_target="tpu_custom_call" | custom-call | tf_op jit(solution)/shard_map/pallas_call | solution.py:312
  66.7 1.3 %copy.9 = f32[4,256]{1,0:T(4,128)} copy(f32[4,256]{1,0:T(4,128)} %get-tuple-element.4) | data formatting | bytes 8192
  67.9 1.2 %copy.10 = f32[4,10]{1,0:T(4,128)} copy(f32[4,10]{1,0:T(4,128)} %get-tuple-element.5) | data formatting | bytes 320

commit v5 on v4

--- a/solution.py
+++ b/solution.py
@@ -9,25 +9,25 @@
 
 MESH = pl.DeviceIdType.MESH
 TOPN = 10
-REACH = 4
-LAG = 15
+REACH = 6
+LAG = 13
 ORDER = [
-    [1, 2, 3, 4, 5, 15, 6, 7, 11, 9, 8, 13, 12, 10, 14],
-    [3, 7, 9, 8, 6, 4, 5, 10, 12, 11, 13, 0, 14, 15, 2],
-    [1, 4, 7, 6, 9, 8, 3, 10, 5, 0, 11, 12, 13, 14, 15],
-    [1, 2, 9, 6, 8, 0, 5, 4, 10, 11, 13, 12, 14, 7, 15],
-    [1, 2, 3, 0, 8, 9, 5, 7, 10, 11, 6, 12, 13, 14, 15],
-    [1, 2, 3, 4, 7, 0, 8, 6, 9, 10, 11, 12, 13, 14, 15],
-    [1, 2, 3, 4, 5, 0, 9, 8, 10, 7, 11, 12, 13, 14, 15],
-    [1, 2, 3, 4, 5, 8, 6, 0, 9, 10, 11, 13, 14, 15, 12],
-    [1, 2, 3, 5, 4, 9, 6, 7, 0, 11, 10, 12, 13, 14, 15],
-    [1, 2, 3, 8, 5, 4, 6, 7, 0, 13, 11, 10, 12, 14, 15],
-    [1, 2, 3, 4, 5, 12, 6, 7, 11, 0, 8, 9, 13, 14, 15],
-    [1, 2, 3, 13, 4, 5, 0, 6, 7, 12, 10, 8, 9, 14, 15],
-    [1, 2, 3, 4, 5, 0, 6, 7, 10, 8, 9, 11, 14, 13, 15],
-    [1, 2, 3, 0, 4, 14, 5, 6, 7, 12, 8, 9, 11, 15, 10],
-    [1, 2, 0, 3, 4, 5, 6, 7, 12, 8, 9, 11, 13, 10, 15],
-    [0, 1, 2, 3, 4, 5, 6, 7, 8, 9, 11, 10, 12, 13, 14],
+    [9, 1, 4, 13, 10, 5, 2, 3, 11, 15, 8, 6, 7, 14, 12],
+    [5, 6, 9, 7, 2, 8, 10, 3, 4, 12, 11, 13, 0, 14, 15],
+    [1, 5, 10, 9, 3, 11, 13, 7, 12, 6, 14, 15, 0, 4, 8],
+    [1, 2, 7, 10, 5, 4, 0, 8, 6, 11, 13, 12, 14, 15, 9],
+    [1, 2, 3, 5, 10, 9, 0, 8, 11, 12, 13, 7, 14, 15, 6],
+    [1, 2, 3, 4, 9, 6, 0, 8, 7, 12, 13, 10, 14, 15, 11],
+    [1, 2, 3, 4, 5, 9, 10, 7, 0, 11, 12, 14, 15, 8, 13],
+    [1, 2, 3, 4, 5, 6, 0, 8, 13, 11, 12, 10, 9, 14, 15],
+    [1, 2, 3, 4, 5, 7, 6, 10, 0, 9, 11, 13, 12, 14, 15],
+    [1, 2, 3, 4, 5, 6, 7, 8, 0, 10, 15, 11, 12, 14, 13],
+    [1, 2, 3, 4, 5, 6, 7, 8, 9, 14, 0, 15, 13, 12, 11],
+    [1, 2, 3, 4, 5, 6, 7, 8, 9, 10, 0, 12, 14, 13, 15],
+    [1, 2, 3, 4, 5, 0, 6, 7, 8, 9, 10, 11, 14, 15, 13],
+    [1, 0, 2, 3, 4, 5, 6, 7, 8, 9, 10, 11, 12, 14, 15],
+    [0, 1, 2, 3, 4, 5, 6, 7, 8, 9, 10, 11, 15, 12, 13],
+    [0, 1, 2, 3, 4, 5, 6, 7, 8, 9, 10, 11, 12, 13, 14],
 ]
 F32 = jnp.float32
 BF16 = jnp.bfloat16
@@ -61,8 +61,8 @@
 
 
 def kernel(
-    n, q_ref, p_hbm, len_ref, slot_ref, cand_ref, score_ref, top_ref,
-    own, held, stored, weights, best, outgoing, table, load_sem, up_send, down_send, recv_sem, back_send, back_recv, here,
+    n, q_ref, p_hbm, len_ref, table,
+    own, held, stored, weights, best, outgoing, load_sem, up_send, down_send, recv_sem, back_send, back_recv, here,
 ):
     me = lax.axis_index("blk")
     count, span, width = p_hbm.shape
@@ -98,6 +98,12 @@
             device_id={"blk": k}, device_id_type=MESH,
         )
 
+    def to_bottom(k):
+        return pltpu.make_async_remote_copy(
+            src_ref=held.at[k], dst_ref=held.at[k], send_sem=down_send.at[k], recv_sem=recv_sem.at[k],
+            device_id={"blk": 0}, device_id_type=MESH,
+        )
+
     def back(k):
         return pltpu.make_async_remote_copy(
             src_ref=outgoing.at[k], dst_ref=table.at[me], send_sem=back_send.at[k], recv_sem=back_recv.at[me],
@@ -138,12 +144,6 @@
             direct(jnp.int32(1)).start()
 
         loop(near, me, lambda k: direct(k).start())
-
-    cand = jnp.concatenate(
-        [cand_ref[q : q + 1, h * 128 : (h + 1) * 128] for q in range(queries_here) for h in range(2)], axis=0
-    )
-    rows = gather_rows(slot_ref[...], cand // 128, cand % 128)
-    query_of = lax.broadcasted_iota(jnp.int32, rows.shape, 0) // 2
 
     for load in loads:
         load.wait()
@@ -196,6 +196,7 @@
     table[me] = score_block(own[...])
 
     source_at = picked_by(ORDER, me)
+    met = ORDER[1].index(0)
 
     def answer(k):
         outgoing[k] = score_block(held[k])
@@ -228,9 +229,19 @@
             k = source_at(t)
             arrived(k)
 
-            @pl.when(k == 0)
+            @pl.when((k == 0) & (me - 1 <= REACH))
             def _():
                 direct(k).start()
+
+            @pl.when((k == 0) & (me == 1))
+            def _():
+                for far in ORDER[1][:met]:
+                    if far - 1 > REACH:
+                        to_bottom(jnp.int32(far)).start()
+
+            @pl.when((t > met) & (me == 1) & (k - 1 > REACH))
+            def _():
+                to_bottom(k).start()
 
             @pl.when((t == 0) & (me > 1) & (me < last))
             def _():
@@ -250,6 +261,40 @@
 
     loop(0, me, landed)
     loop(me + 1, n, landed)
+
+    @pl.when((me > 0) & (me < last))
+    def _():
+        loop(1, me, lambda k: climb(k, held.at[k]).wait_send())
+        climb(me, own).wait_send()
+        loop(me + REACH + 2, n, lambda k: climb(k, held.at[k]).wait_send())
+
+    @pl.when(me == 0)
+    def _():
+        loop(1, n, lambda k: direct(k).wait_send())
+
+    @pl.when(me == 1)
+    def _():
+        loop(REACH + 2, n, lambda k: to_bottom(k).wait_send())
+
+    @pl.when(me > 0)
+    def _():
+        direct(jnp.where(me - 1 > REACH, 1, 0)).wait_send()
+
+        loop(near, me, lambda k: direct(k).wait_send())
+
+    loop(0, me, lambda k: back(k).wait_send())
+    loop(me + 1, n, lambda k: back(k).wait_send())
+
+
+def finish(slot_ref, cand_ref, table, score_ref, top_ref):
+    n, _, cols = table.shape
+    queries_here = cand_ref.shape[0]
+    tokens = cols // queries_here
+    cand = jnp.concatenate(
+        [cand_ref[q : q + 1, h * 128 : (h + 1) * 128] for q in range(queries_here) for h in range(2)], axis=0
+    )
+    rows = gather_rows(slot_ref[...], cand // 128, cand % 128)
+    query_of = lax.broadcasted_iota(jnp.int32, rows.shape, 0) // 2
 
     lines = table[...].reshape(2 * n, cols)
     score = gather_rows(lines, rows // tokens, query_of * tokens + rows % tokens)
@@ -280,49 +325,17 @@
         line = jnp.sum(jnp.where(spot, total, 0.0), axis=0, keepdims=True)
         top_ref[q : q + 1, :] = line[:, 0:TOPN]
 
-    @pl.when((me > 0) & (me < last))
-    def _():
-        loop(1, me, lambda k: climb(k, held.at[k]).wait_send())
-        climb(me, own).wait_send()
-        loop(me + REACH + 2, n, lambda k: climb(k, held.at[k]).wait_send())
-
-    @pl.when(me == 0)
-    def _():
-        loop(1, n, lambda k: direct(k).wait_send())
-
-    @pl.when(me > 0)
-    def _():
-        direct(jnp.int32(0)).wait_send()
-
-        @pl.when(me - 1 > REACH)
-        def _():
-            direct(jnp.int32(1)).wait_send()
-
-        loop(near, me, lambda k: direct(k).wait_send())
-
-    loop(0, me, lambda k: back(k).wait_send())
-    loop(me + 1, n, lambda k: back(k).wait_send())
-
 
 def shards(n, queries, passages, lengths, slot_of, candidates):
     queries_here, tokens, width = queries.shape
     count, span, _ = passages.shape
     cols = queries_here * tokens
     vmem = pl.BlockSpec(memory_space=pltpu.VMEM)
-    return pl.pallas_call(
+    scores = pl.pallas_call(
         functools.partial(kernel, n),
-        out_shape=(
-            jax.ShapeDtypeStruct(candidates.shape, F32),
-            jax.ShapeDtypeStruct((queries_here, TOPN), F32),
-        ),
-        in_specs=[
-            vmem,
-            pl.BlockSpec(memory_space=pl.ANY),
-            pl.BlockSpec(memory_space=pltpu.SMEM),
-            vmem,
-            vmem,
-        ],
-        out_specs=(vmem, vmem),
+        out_shape=jax.ShapeDtypeStruct((n, 2, cols), F32),
+        in_specs=[vmem, pl.BlockSpec(memory_space=pl.ANY), pl.BlockSpec(memory_space=pltpu.SMEM)],
+        out_specs=vmem,
         scratch_shapes=[
             pltpu.VMEM((width, cols), BF16),
             pltpu.VMEM((n, width, cols), BF16),
@@ -330,7 +343,6 @@
             pltpu.VMEM((2 * width, 2 * cols), BF16),
             pltpu.VMEM((count // 2, 2 * cols), F32),
             pltpu.VMEM((n, 2, cols), F32),
-            pltpu.VMEM((n, 2, cols), F32),
             pltpu.SemaphoreType.DMA((2,)),
             pltpu.SemaphoreType.DMA((n,)),
             pltpu.SemaphoreType.DMA((n,)),
@@ -340,7 +352,16 @@
             pltpu.SemaphoreType.REGULAR,
         ],
         compiler_params=pltpu.CompilerParams(collective_id=0, has_side_effects=True),
-    )(queries, passages, lengths, slot_of.reshape(-1, 128), candidates)
+    )(queries, passages, lengths)
+    return pl.pallas_call(
+        finish,
+        out_shape=(
+            jax.ShapeDtypeStruct(candidates.shape, F32),
+            jax.ShapeDtypeStruct((queries_here, TOPN), F32),
+        ),
+        in_specs=[vmem] * 3,
+        out_specs=(vmem, vmem),
+    )(slot_of.reshape(-1, 128), candidates, scores)
 
 
 def solution(mesh):

time: 69.5 us -> 71.1 us (1.023)
  Pallas kernels: 66 us -> 70.1 us
  local copies, waits for them, and re-layouts: 2.5 us -> 0 us
    pallas_call x1 -> x2, Pallas kernels: 66 us -> 70.1 us  [the longest x1 68.2 us: shards(): pl.pallas_call(functools.partial(kernel, n), out_shape=jax.ShapeDtypeStru...]
    unnamed x2 -> x0, local copies, waits for them, and re-layouts: 2.5 us -> none
where the time goes in v5:
time: 71.1 us; the launch traced here: 70.8 us
  Pallas kernels  70.1 us (99%)
    pallas_call x1, Pallas kernels, shards(): pl.pallas_call(functools.partial(kernel, n), out_shape=jax.ShapeDtypeStru...  68.2 us
    pallas_call x1, Pallas kernels, shards(): pl.pallas_call(finish, out_shape=(jax.ShapeDtypeStruct(candidates.shape,...  1.95 us

profile of v5, /device:TPU:78, one launch (start us, length us, event | category | flops | bytes accessed | tf_op | source)
XLA Modules:
  0.0 70.8 jit_solution(2411345731102351716)
XLA Ops:
  0.6 68.2 %shard_map.68.table = f32[16,2,128]{2,1,0:T(2,128)} custom-call(bf16[4,32,128]{2,1,0:T(8,128)(2,1)} %q_ref.1, bf16[64,128,128]{2,1,0:T(8,128)(2,1)} %p_hbm.1, s32[64]{0:T(128)} %len_ref.1), custom_call_target="tpu_custom_call" | custom-call | tf_op jit(solution)/shard_map/pallas_call | solution.py:334
  68.8 1.9 %shard_map.69 = (f32[4,256]{1,0:T(4,128)}, f32[4,10]{1,0:T(4,128)}) custom-call(s32[8,128]{1,0:T(8,128)} %bitcast.1, s32[4,256]{1,0:T(4,128)} %cand_ref.1, f32[16,2,128]{2,1,0:T(2,128)} %shard_map.68.table), custom_call_target="tpu_custom_call" | custom-call | tf_op jit(solution)/shard_map/pallas_call | solution.py:356

commit v6 on v5

--- a/solution.py
+++ b/solution.py
@@ -9,25 +9,25 @@
 
 MESH = pl.DeviceIdType.MESH
 TOPN = 10
-REACH = 6
-LAG = 13
+REACH = 4
+LAG = 15
 ORDER = [
-    [9, 1, 4, 13, 10, 5, 2, 3, 11, 15, 8, 6, 7, 14, 12],
-    [5, 6, 9, 7, 2, 8, 10, 3, 4, 12, 11, 13, 0, 14, 15],
-    [1, 5, 10, 9, 3, 11, 13, 7, 12, 6, 14, 15, 0, 4, 8],
-    [1, 2, 7, 10, 5, 4, 0, 8, 6, 11, 13, 12, 14, 15, 9],
-    [1, 2, 3, 5, 10, 9, 0, 8, 11, 12, 13, 7, 14, 15, 6],
-    [1, 2, 3, 4, 9, 6, 0, 8, 7, 12, 13, 10, 14, 15, 11],
-    [1, 2, 3, 4, 5, 9, 10, 7, 0, 11, 12, 14, 15, 8, 13],
-    [1, 2, 3, 4, 5, 6, 0, 8, 13, 11, 12, 10, 9, 14, 15],
-    [1, 2, 3, 4, 5, 7, 6, 10, 0, 9, 11, 13, 12, 14, 15],
-    [1, 2, 3, 4, 5, 6, 7, 8, 0, 10, 15, 11, 12, 14, 13],
-    [1, 2, 3, 4, 5, 6, 7, 8, 9, 14, 0, 15, 13, 12, 11],
-    [1, 2, 3, 4, 5, 6, 7, 8, 9, 10, 0, 12, 14, 13, 15],
-    [1, 2, 3, 4, 5, 0, 6, 7, 8, 9, 10, 11, 14, 15, 13],
-    [1, 0, 2, 3, 4, 5, 6, 7, 8, 9, 10, 11, 12, 14, 15],
-    [0, 1, 2, 3, 4, 5, 6, 7, 8, 9, 10, 11, 15, 12, 13],
-    [0, 1, 2, 3, 4, 5, 6, 7, 8, 9, 10, 11, 12, 13, 14],
+    [1, 2, 3, 4, 5, 15, 6, 7, 11, 9, 8, 13, 12, 10, 14],
+    [3, 7, 9, 8, 6, 4, 5, 10, 12, 11, 13, 0, 14, 15, 2],
+    [1, 4, 7, 6, 9, 8, 3, 10, 5, 0, 11, 12, 13, 14, 15],
+    [1, 2, 9, 6, 8, 0, 5, 4, 10, 11, 13, 12, 14, 7, 15],
+    [1, 2, 3, 0, 8, 9, 5, 7, 10, 11, 6, 12, 13, 14, 15],
+    [1, 2, 3, 4, 7, 0, 8, 6, 9, 10, 11, 12, 13, 14, 15],
+    [1, 2, 3, 4, 5, 0, 9, 8, 10, 7, 11, 12, 13, 14, 15],
+    [1, 2, 3, 4, 5, 8, 6, 0, 9, 10, 11, 13, 14, 15, 12],
+    [1, 2, 3, 5, 4, 9, 6, 7, 0, 11, 10, 12, 13, 14, 15],
+    [1, 2, 3, 8, 5, 4, 6, 7, 0, 13, 11, 10, 12, 14, 15],
+    [1, 2, 3, 4, 5, 12, 6, 7, 11, 0, 8, 9, 13, 14, 15],
+    [1, 2, 3, 13, 4, 5, 0, 6, 7, 12, 10, 8, 9, 14, 15],
+    [1, 2, 3, 4, 5, 0, 6, 7, 10, 8, 9, 11, 14, 13, 15],
+    [1, 2, 3, 0, 4, 14, 5, 6, 7, 12, 8, 9, 11, 15, 10],
+    [1, 2, 0, 3, 4, 5, 6, 7, 12, 8, 9, 11, 13, 10, 15],
+    [0, 1, 2, 3, 4, 5, 6, 7, 8, 9, 11, 10, 12, 13, 14],
 ]
 F32 = jnp.float32
 BF16 = jnp.bfloat16
@@ -96,12 +96,6 @@
         return pltpu.make_async_remote_copy(
             src_ref=own, dst_ref=held.at[me], send_sem=down_send.at[k], recv_sem=recv_sem.at[me],
             device_id={"blk": k}, device_id_type=MESH,
-        )
-
-    def to_bottom(k):
-        return pltpu.make_async_remote_copy(
-            src_ref=held.at[k], dst_ref=held.at[k], send_sem=down_send.at[k], recv_sem=recv_sem.at[k],
-            device_id={"blk": 0}, device_id_type=MESH,
         )
 
     def back(k):
@@ -196,7 +190,6 @@
     table[me] = score_block(own[...])
 
     source_at = picked_by(ORDER, me)
-    met = ORDER[1].index(0)
 
     def answer(k):
         outgoing[k] = score_block(held[k])
@@ -229,19 +222,9 @@
             k = source_at(t)
             arrived(k)
 
-            @pl.when((k == 0) & (me - 1 <= REACH))
+            @pl.when(k == 0)
             def _():
                 direct(k).start()
-
-            @pl.when((k == 0) & (me == 1))
-            def _():
-                for far in ORDER[1][:met]:
-                    if far - 1 > REACH:
-                        to_bottom(jnp.int32(far)).start()
-
-            @pl.when((t > met) & (me == 1) & (k - 1 > REACH))
-            def _():
-                to_bottom(k).start()
 
             @pl.when((t == 0) & (me > 1) & (me < last))
             def _():
@@ -272,13 +255,13 @@
     def _():
         loop(1, n, lambda k: direct(k).wait_send())
 
-    @pl.when(me == 1)
-    def _():
-        loop(REACH + 2, n, lambda k: to_bottom(k).wait_send())
-
     @pl.when(me > 0)
     def _():
-        direct(jnp.where(me - 1 > REACH, 1, 0)).wait_send()
+        direct(jnp.int32(0)).wait_send()
+
+        @pl.when(me - 1 > REACH)
+        def _():
+            direct(jnp.int32(1)).wait_send()
 
         loop(near, me, lambda k: direct(k).wait_send())
 

time: 71.1 us -> 68.9 us (0.969)
  Pallas kernels: 70.1 us -> 68 us
    pallas_call x1, Pallas kernels: 68.2 us -> 66 us  [shards(): pl.pallas_call(functools.partial(kernel, n), out_shape=jax.ShapeDtypeStru...]
where the time goes in v6:
time: 68.9 us; the launch traced here: 68.6 us
  Pallas kernels  68 us (99%)
    pallas_call x1, Pallas kernels, shards(): pl.pallas_call(functools.partial(kernel, n), out_shape=jax.ShapeDtypeStru...  66 us
    pallas_call x1, Pallas kernels, shards(): pl.pallas_call(finish, out_shape=(jax.ShapeDtypeStruct(candidates.shape,...  1.95 us

profile of v6, /device:TPU:78, one launch (start us, length us, event | category | flops | bytes accessed | tf_op | source)
XLA Modules:
  0.0 68.6 jit_solution(15905015117377885199)
XLA Ops:
  0.6 66.0 %shard_map.68.table = f32[16,2,128]{2,1,0:T(2,128)} custom-call(bf16[4,32,128]{2,1,0:T(8,128)(2,1)} %q_ref.1, bf16[64,128,128]{2,1,0:T(8,128)(2,1)} %p_hbm.1, s32[64]{0:T(128)} %len_ref.1), custom_call_target="tpu_custom_call" | custom-call | tf_op jit(solution)/shard_map/pallas_call | solution.py:317
  66.7 1.9 %shard_map.69 = (f32[4,256]{1,0:T(4,128)}, f32[4,10]{1,0:T(4,128)}) custom-call(s32[8,128]{1,0:T(8,128)} %bitcast.1, s32[4,256]{1,0:T(4,128)} %cand_ref.1, f32[16,2,128]{2,1,0:T(2,128)} %shard_map.68.table), custom_call_target="tpu_custom_call" | custom-call | tf_op jit(solution)/shard_map/pallas_call | solution.py:339

commit v7 on v6

--- a/solution.py
+++ b/solution.py
@@ -9,25 +9,25 @@
 
 MESH = pl.DeviceIdType.MESH
 TOPN = 10
-REACH = 4
+REACH = 5
 LAG = 15
 ORDER = [
-    [1, 2, 3, 4, 5, 15, 6, 7, 11, 9, 8, 13, 12, 10, 14],
-    [3, 7, 9, 8, 6, 4, 5, 10, 12, 11, 13, 0, 14, 15, 2],
-    [1, 4, 7, 6, 9, 8, 3, 10, 5, 0, 11, 12, 13, 14, 15],
-    [1, 2, 9, 6, 8, 0, 5, 4, 10, 11, 13, 12, 14, 7, 15],
-    [1, 2, 3, 0, 8, 9, 5, 7, 10, 11, 6, 12, 13, 14, 15],
-    [1, 2, 3, 4, 7, 0, 8, 6, 9, 10, 11, 12, 13, 14, 15],
-    [1, 2, 3, 4, 5, 0, 9, 8, 10, 7, 11, 12, 13, 14, 15],
-    [1, 2, 3, 4, 5, 8, 6, 0, 9, 10, 11, 13, 14, 15, 12],
-    [1, 2, 3, 5, 4, 9, 6, 7, 0, 11, 10, 12, 13, 14, 15],
-    [1, 2, 3, 8, 5, 4, 6, 7, 0, 13, 11, 10, 12, 14, 15],
-    [1, 2, 3, 4, 5, 12, 6, 7, 11, 0, 8, 9, 13, 14, 15],
-    [1, 2, 3, 13, 4, 5, 0, 6, 7, 12, 10, 8, 9, 14, 15],
-    [1, 2, 3, 4, 5, 0, 6, 7, 10, 8, 9, 11, 14, 13, 15],
-    [1, 2, 3, 0, 4, 14, 5, 6, 7, 12, 8, 9, 11, 15, 10],
-    [1, 2, 0, 3, 4, 5, 6, 7, 12, 8, 9, 11, 13, 10, 15],
-    [0, 1, 2, 3, 4, 5, 6, 7, 8, 9, 11, 10, 12, 13, 14],
+    [15, 4, 1, 2, 13, 6, 3, 9, 7, 14, 5, 8, 10, 12, 11],
+    [3, 6, 7, 10, 4, 8, 11, 2, 9, 14, 12, 0, 13, 5, 15],
+    [1, 5, 10, 9, 6, 4, 3, 7, 0, 11, 12, 13, 8, 14, 15],
+    [1, 2, 6, 5, 8, 4, 0, 9, 7, 10, 11, 13, 14, 15, 12],
+    [1, 2, 3, 6, 9, 0, 8, 10, 5, 7, 11, 13, 14, 15, 12],
+    [1, 2, 3, 4, 7, 6, 8, 0, 10, 11, 13, 14, 15, 9, 12],
+    [1, 2, 3, 5, 4, 0, 10, 8, 11, 13, 9, 14, 15, 7, 12],
+    [1, 2, 3, 5, 4, 6, 12, 10, 0, 8, 13, 11, 14, 15, 9],
+    [1, 2, 3, 5, 4, 7, 6, 0, 12, 10, 11, 13, 9, 14, 15],
+    [1, 2, 3, 8, 5, 4, 12, 13, 11, 6, 7, 0, 10, 14, 15],
+    [1, 2, 3, 12, 5, 4, 6, 7, 8, 0, 9, 13, 11, 14, 15],
+    [13, 1, 2, 3, 5, 4, 10, 6, 7, 0, 8, 9, 14, 12, 15],
+    [1, 2, 3, 0, 4, 5, 6, 7, 10, 8, 9, 11, 13, 15, 14],
+    [14, 0, 1, 2, 3, 4, 5, 6, 7, 8, 9, 10, 11, 12, 15],
+    [0, 1, 2, 3, 13, 4, 5, 6, 7, 8, 9, 10, 11, 12, 15],
+    [0, 1, 2, 3, 4, 5, 6, 7, 8, 9, 10, 11, 12, 14, 13],
 ]
 F32 = jnp.float32
 BF16 = jnp.bfloat16

time: 68.9 us -> 72.9 us (1.058)
  Pallas kernels: 68 us -> 72 us
    pallas_call x1, Pallas kernels: 66 us -> 70.1 us  [shards(): pl.pallas_call(functools.partial(kernel, n), out_shape=jax.ShapeDtypeStru...]
where the time goes in v7:
time: 72.9 us; the launch traced here: 72.7 us
  Pallas kernels  72 us (99%)
    pallas_call x1, Pallas kernels, shards(): pl.pallas_call(functools.partial(kernel, n), out_shape=jax.ShapeDtypeStru...  70.1 us
    pallas_call x1, Pallas kernels, shards(): pl.pallas_call(finish, out_shape=(jax.ShapeDtypeStruct(candidates.shape,...  1.95 us

profile of v7, /device:TPU:78, one launch (start us, length us, event | category | flops | bytes accessed | tf_op | source)
XLA Modules:
  0.0 72.7 jit_solution(17615366180969513430)
XLA Ops:
  0.6 70.1 %shard_map.68.table = f32[16,2,128]{2,1,0:T(2,128)} custom-call(bf16[4,32,128]{2,1,0:T(8,128)(2,1)} %q_ref.1, bf16[64,128,128]{2,1,0:T(8,128)(2,1)} %p_hbm.1, s32[64]{0:T(128)} %len_ref.1), custom_call_target="tpu_custom_call" | custom-call | tf_op jit(solution)/shard_map/pallas_call | solution.py:317
  70.7 1.9 %shard_map.69 = (f32[4,256]{1,0:T(4,128)}, f32[4,10]{1,0:T(4,128)}) custom-call(s32[8,128]{1,0:T(8,128)} %bitcast.1, s32[4,256]{1,0:T(4,128)} %cand_ref.1, f32[16,2,128]{2,1,0:T(2,128)} %shard_map.68.table), custom_call_target="tpu_custom_call" | custom-call | tf_op jit(solution)/shard_map/pallas_call | solution.py:339
